TPU v7x, 128 devices: a whole 4x4x4 slice. The times are simulated.
128 devices in a mesh: copy: 4 (over z), row: 4 (over x_hi, core), col: 8 (over y, x_lo).
Axes of the slice: x: 4 (x_hi: 2, x_lo: 2; x = x_hi * 2 + x_lo), y: 4, z: 4, core: 2. Of those that a mesh axis runs over, the one named last changes fastest.
Arguments:
- trailing: float32 [32768, 16, 8, 128], P(('copy', 'row'), None, 'col'), parts along dimension 0, may hold values from -6 to 6
- lower_trail: float32 [64, 8, 128, 768], P(('copy', 'row'), None, None, 'col'), parts along dimension 0, may hold values from -0.046875 to 0.046875
- lower_cross: float32 [384, 384], replicated, may hold values from -0.3125 to 0.3125
- panel_inverse: float32 [2, 384, 384], replicated, may hold values from -1 to 1, as said below
- target: float32 [32768, 2, 384], P(('copy', 'row'), None, 'col'), parts along dimension 0, may hold values from -6 to 6
Outputs:
- inverse_panels: float32 [32768, 2, 384], P(('copy', 'row'), None, 'col'), parts along dimension 0
There are 4 independent parts, one for each index of `copy`. A program takes and returns all parts, laid end to end along the dimension named above; an argument that names none is the same for every part. Nothing has to cross between parts.
Inputs may be any that keep to these rules, and one draw needn't show every extreme that they name: `panel_inverse`: each of the two 384 x 384 matrices is unit lower triangular: ones on the diagonal, zeros above it.
All inputs are finite; a program needn't handle non-finite values.
Results may differ from a plain program's by a relative error of at most 0.000071.
Values sent between devices are 32-bit elements; how exact they have to be, the bound alone decides.
A program may use at most 192 MiB of HBM per device.

v0:
```python
import jax
import jax.numpy as jnp
from jax import lax
from jax.sharding import PartitionSpec as P

precise = lax.Precision.HIGHEST


def sent_to_all(array, axis):
    count = lax.axis_size(axis)
    return lax.all_to_all(
        jnp.broadcast_to(array[None], (count, *array.shape)), axis, 0, 0, tiled=True
    )


def laid_out(parts, dim):
    lengths = list(parts.shape[1:])
    lengths[dim] *= parts.shape[0]
    return jnp.moveaxis(parts, 0, dim).reshape(lengths)


def collect(array, axis, dim):
    parts = sent_to_all(array, axis)
    return laid_out(parts, dim)


def cut_along(array, dim, count):
    before, after = (array.shape[:dim], array.shape[dim + 1 :])
    return jnp.moveaxis(array.reshape(*before, count, -1, *after), dim, 0)


def sent_and_summed(array, axis, dim):
    count = lax.axis_size(axis)
    parts = lax.all_to_all(cut_along(array, dim, count), axis, 0, 0, tiled=True)
    return jnp.sum(parts, axis=0)


def matmul(first, second):
    return jnp.dot(first, second, preferred_element_type=jnp.float32, precision=precise)


def own_columns(matrix, dim):
    share_cols = matrix.shape[dim] // lax.axis_size("col")
    return lax.dynamic_slice_in_dim(matrix, lax.axis_index("col") * share_cols, share_cols, dim)


def per_device(trailing, lower_trail, lower_cross, panel_inverse, target):
    row_count = trailing.shape[0]
    block_cols = trailing.shape[3]
    trail_flat = trailing.reshape(row_count, trailing.shape[1] * block_cols)
    span_cols = lower_trail.shape[3] * lax.axis_size("col")
    panel_cols = span_cols // 2
    relaid = lax.all_to_all(lower_trail, "col", split_axis=1, concat_axis=3, tiled=True)
    segment = collect(relaid, "row", 0)
    block_count = segment.shape[0]
    update = matmul(trail_flat, segment.reshape(block_count * block_cols, span_cols))
    update = update.reshape(row_count, 2, panel_cols)
    right_sum = sent_and_summed(update[:, 1], "col", 1)
    right_rest = collect(target[:, 1] - right_sum, "col", 1)
    right_panel = matmul(right_rest, panel_inverse[1])
    left_sum = sent_and_summed(update[:, 0], "col", 1)
    left_rest = collect(target[:, 0] - left_sum, "col", 1)
    left_panel = matmul(left_rest - matmul(right_panel, lower_cross), panel_inverse[0])
    return own_columns(jnp.stack([left_panel, right_panel], axis=1), 2)


def solution(mesh):
    placed = (
        P(("copy", "row"), None, "col", None),
        P(("copy", "row"), None, None, "col"),
        P(),
        P(),
        P(("copy", "row"), None, "col"),
    )
    return jax.shard_map(
        per_device,
        mesh=mesh,
        in_specs=placed,
        out_specs=P(("copy", "row"), None, "col"),
        check_vma=False,
    )
```

profile of v0, /device:TPU:0, one launch (start us, length us, event | category | flops | bytes accessed | tf_op | source)
XLA Modules:
  0.0 364.1 jit_solution(2228694661465857541)
XLA Ops:
  0.0 1.6 copy.12
  1.6 26.8 %all_to_all.40 = f32[4,8,128,96]{2,3,0,1:T(8,128)S(1)} all-to-all(f32[4,8,128,96]{2,3,0,1:T(8,128)S(1)} %copy.12), channel_id=1, replica_groups=mesh['copy'=4,'row'=4,'col'=8] {'col'}, dimensions={1} | all-to-all | bytes 3145728 | tf_op jit(solution)/shard_map/all_to_all | solution.py:53
  28.4 0.1 copy.13
  28.6 1.0 copy.14
  29.6 3.4 broadcast_in_dim.9
  33.0 5.2 %all-to-all-start.1 = ((f32[4,4,1,128,768]{3,1,4,2,0:T(4,128)}), f32[4,4,1,128,768]{3,1,4,2,0:T(4,128)}, u32[]{:S(2)}, u32[]{:S(2)}) async-start(f32[4,4,1,128,768]{3,1,4,2,0:T(4,128)} %broadcast_in_dim.9), calls=%async_computation.1 | async-start | bytes 12582912 | tf_op jit(solution)/shard_map/all_to_all | solution.py:11
  38.2 0.5 broadcast.4
  38.7 50.0 %reduce.3 = f32[2048,16,128]{2,1,0:T(8,128)} reduce(f32[2048,16,1,128]{3,2,1,0:T(1,128)} %param.5, f32[]{:T(128)} %broadcast.4), dimensions={2}, to_apply=%param.5.reduce_sub_computation.3 | reduce | bytes 33554436 | tf_op args[0]
  88.8 18.0 %reshape.32 = f32[2048,2048,1]{1,0,2:T(8,128)} reshape(f32[2048,16,128]{2,1,0:T(8,128)} %reduce.3) | data formatting | bytes 33554432 | tf_op jit(solution)/shard_map/reshape | solution.py:50
  106.7 3.7 %all-to-all-done.1 = f32[4,4,1,128,768]{3,1,4,2,0:T(4,128)} async-done(((f32[4,4,1,128,768]{3,1,4,2,0:T(4,128)}), f32[4,4,1,128,768]{3,1,4,2,0:T(4,128)}, u32[]{:S(2)}, u32[]{:S(2)}) %all-to-all-start.1) | async-done | bytes 6291488 | tf_op jit(solution)/shard_map/all_to_all | solution.py:11
  110.4 7.6 %copy.15 = f32[4,4,1,128,768]{4,3,1,0,2:T(8,128)} copy(f32[4,4,1,128,768]{3,1,4,2,0:T(4,128)} %all-to-all-done.1) | data formatting | bytes 12582912 | tf_op jit(solution)/shard_map/all_to_all | solution.py:11
  118.1 6.6 %copy.16 = f32[768,2048]{1,0:T(8,128)} copy(f32[768,2048]{0,1:T(8,128)} %bitcast.40) | data formatting | bytes 12582912 | tf_op jit(solution)/shard_map/dot_general | solution.py:39
  124.6 45.8 %fusion.12 = f32[2048,2,384]{0,2,1:T(8,128)S(1)} fusion(f32[2048,2048,1]{1,0,2:T(8,128)} %reshape.32, f32[2,384,2048]{2,1,0:T(8,128)} %bitcast.44), kind=kOutput, calls=%fused_computation.14 | convolution fusion | flops 38654705664 | bytes 29360128 | tf_op jit(solution)/shard_map/dot_general | solution.py:39
  170.4 2.2 fusion.11
  172.6 41.8 %all_to_all.41 = f32[8,2048,48]{1,2,0:T(8,128)} all-to-all(f32[8,2048,48]{1,2,0:T(8,128)S(1)} %bitcast.43), channel_id=1, replica_groups=mesh['copy'=4,'row'=4,'col'=8] {'col'}, dimensions={0} | all-to-all | bytes 6291456 | tf_op jit(solution)/shard_map/all_to_all | solution.py:34
  214.5 4.5 %all-to-all-start.4 = ((f32[8,2048,48]{1,2,0:T(8,128)}), f32[8,2048,48]{1,2,0:T(8,128)}, u32[]{:S(2)}, u32[]{:S(2)}) async-start(f32[8,2048,48]{1,2,0:T(8,128)} %bitcast.42), calls=%async_computation.4 | async-start | bytes 6291456 | tf_op jit(solution)/shard_map/all_to_all | solution.py:34
  218.9 0.0 copy-start.3
  218.9 2.2 reduce_sum.18
  221.1 35.2 %all-to-all-done.4 = f32[8,2048,48]{1,2,0:T(8,128)} async-done(((f32[8,2048,48]{1,2,0:T(8,128)}), f32[8,2048,48]{1,2,0:T(8,128)}, u32[]{:S(2)}, u32[]{:S(2)}) %all-to-all-start.4) | async-done | bytes 3145760 | tf_op jit(solution)/shard_map/all_to_all | solution.py:34
  256.3 2.1 reduce_sum.19
  258.4 0.1 bitcast_subtract_fusion
  258.5 0.4 broadcast_in_dim.10
  258.8 40.9 %all_to_all.42 = f32[8,2048,48]{1,2,0:T(8,128)} all-to-all(f32[8,2048,48]{1,2,0:T(8,128)S(1)} %broadcast_in_dim.10), channel_id=1, replica_groups=mesh['copy'=4,'row'=4,'col'=8] {'col'}, dimensions={0} | all-to-all | bytes 6291456 | tf_op jit(solution)/shard_map/all_to_all | solution.py:11
  299.7 2.0 broadcast_in_dim.11
  301.8 4.5 %all-to-all-start.5 = ((f32[8,2048,48]{1,2,0:T(8,128)}), f32[8,2048,48]{1,2,0:T(8,128)}, u32[]{:S(2)}, u32[]{:S(2)}) async-start(f32[8,2048,48]{1,2,0:T(8,128)} %broadcast_in_dim.11), calls=%async_computation.5 | async-start | bytes 6291456 | tf_op jit(solution)/shard_map/all_to_all | solution.py:11
  306.2 0.0 copy-start.2
  306.2 3.9 %copy.17 = f32[2048,384]{1,0:T(8,128)} copy(f32[2048,384]{0,1:T(8,128)} %bitcast.41) | data formatting | bytes 6291456 | tf_op jit(solution)/shard_map/reshape | solution.py:19
  310.1 33.0 %all-to-all-done.5 = f32[8,2048,48]{1,2,0:T(8,128)} async-done(((f32[8,2048,48]{1,2,0:T(8,128)}), f32[8,2048,48]{1,2,0:T(8,128)}, u32[]{:S(2)}, u32[]{:S(2)}) %all-to-all-start.5) | async-done | bytes 3145760 | tf_op jit(solution)/shard_map/all_to_all | solution.py:11
  343.1 7.3 %fusion.7 = f32[2048,384]{0,1:T(8,128)S(1)} fusion(f32[2048,384]{0,1:T(8,128)} %bitcast.15, f32[2,384,384]{2,1,0:T(8,128)S(1)} %copy-done.2), kind=kOutput, calls=%fused_computation.7 | convolution fusion | flops 3623878656 | bytes 6881280 | tf_op jit(solution)/shard_map/dot_general | solution.py:39
  350.4 6.5 %fusion.13 = f32[2048,384]{1,0:T(8,128)S(1)} fusion(f32[2048,384]{0,1:T(8,128)S(1)} %fusion.7, f32[384,384]{1,0:T(8,128)S(1)} %copy-done), kind=kOutput, calls=%fused_computation.15 | convolution fusion | flops 3623878656 | bytes 6881280 | tf_op jit(solution)/shard_map/dot_general | solution.py:39
  357.0 5.7 %fusion.2 = f32[2048,1,384]{0,2,1:T(8,128)S(1)} fusion(f32[2048,384]{1,0:T(8,128)S(1)} %copy-done.1, f32[2048,384]{1,0:T(8,128)S(1)} %fusion.13, f32[2,384,384]{2,1,0:T(8,128)S(1)} %copy-done.2), kind=kOutput, calls=%fused_computation.4 | convolution fusion | flops 3624665088 | bytes 10027008 | tf_op jit(solution)/shard_map/dot_general | solution.py:39
  362.8 0.9 fusion.5
  (6 shorter events, 0.0 us)
Async XLA Ops:
  0.0 350.4 %copy-start = (f32[384,384]{1,0:T(8,128)S(1)}, f32[384,384]{1,0:T(8,128)}, u32[]{:S(2)}) copy-start(f32[384,384]{1,0:T(8,128)} %param.7) | copy-start | bytes 1769476
  33.0 77.4 %all-to-all-start.1 = ((f32[4,4,1,128,768]{3,1,4,2,0:T(4,128)}), f32[4,4,1,128,768]{3,1,4,2,0:T(4,128)}, u32[]{:S(2)}, u32[]{:S(2)}) async-start(f32[4,4,1,128,768]{3,1,4,2,0:T(4,128)} %broadcast_in_dim.9), calls=%async_computation.1 | async-start | bytes 12582912 | tf_op jit(solution)/shard_map/all_to_all | solution.py:11
  214.5 41.8 %all-to-all-start.4 = ((f32[8,2048,48]{1,2,0:T(8,128)}), f32[8,2048,48]{1,2,0:T(8,128)}, u32[]{:S(2)}, u32[]{:S(2)}) async-start(f32[8,2048,48]{1,2,0:T(8,128)} %bitcast.42), calls=%async_computation.4 | async-start | bytes 6291456 | tf_op jit(solution)/shard_map/all_to_all | solution.py:34
  218.9 39.4 %copy-start.3 = (f32[2048,2,48]{0,2,1:T(8,128)S(1)}, f32[2048,2,48]{0,2,1:T(8,128)}, u32[]{:S(2)}) copy-start(f32[2048,2,48]{0,2,1:T(8,128)} %param.9) | copy-start | bytes 2359300
  301.8 41.4 %all-to-all-start.5 = ((f32[8,2048,48]{1,2,0:T(8,128)}), f32[8,2048,48]{1,2,0:T(8,128)}, u32[]{:S(2)}, u32[]{:S(2)}) async-start(f32[8,2048,48]{1,2,0:T(8,128)} %broadcast_in_dim.11), calls=%async_computation.5 | async-start | bytes 6291456 | tf_op jit(solution)/shard_map/all_to_all | solution.py:11
  306.2 36.9 %copy-start.2 = (f32[2,384,384]{2,1,0:T(8,128)S(1)}, f32[2,384,384]{2,1,0:T(8,128)}, u32[]{:S(2)}) copy-start(f32[2,384,384]{2,1,0:T(8,128)} %param.8) | copy-start | bytes 3538948
  350.4 6.5 %copy-start.1 = (f32[2048,384]{1,0:T(8,128)S(1)}, f32[2048,384]{1,0:T(8,128)}, u32[]{:S(2)}) copy-start(f32[2048,384]{1,0:T(8,128)} %copy.17) | copy-start | bytes 9437188
where the time goes:
time: 370 us; the launch traced here: 364 us
  blocking collectives  110 us (30%)
  waiting for transfers between devices  71.8 us (19%)
  matrix products  65.3 us (18%)
  other arithmetic  55.3 us (15%)
  local copies, waits for them, and re-layouts  47.3 us (13%)
  starting transfers between devices  14.1 us (4%)
    dot_general x4, matrix products, matmul(): jnp.dot(first, second, preferred_element_type=jnp.float32, precision=prec...  65.3 us
    unnamed x1, other arithmetic  50 us
    all_to_all x1, blocking collectives, sent_and_summed(): parts = lax.all_to_all(cut_along(array, dim, count), axis, 0, 0, tiled=True)  41.8 us
    all_to_all x1, blocking collectives, sent_to_all(): lax.all_to_all(jnp.broadcast_to(array[None], (count, *array.shape)), axis...  40.9 us
    all_to_all x2, waiting for transfers between devices, sent_to_all(): lax.all_to_all(jnp.broadcast_to(array[None], (count, *array.shape)), axis...  36.7 us
    all_to_all x1, waiting for transfers between devices, sent_and_summed(): parts = lax.all_to_all(cut_along(array, dim, count), axis, 0, 0, tiled=True)  35.2 us
    all_to_all x1, blocking collectives, per_device(): lax.all_to_all(lower_trail, 'col', split_axis=1, concat_axis=3, tiled=True)  26.8 us
    reshape x1, local copies, waits for them, and re-layouts, per_device(): trail_flat = trailing.reshape(row_count, trailing.shape[1] * block_cols)  18 us
  transfers between devices with their start and end apart: 3, of which 3 were waited for; matrix products, arithmetic and copies ran while one was open for 20% of the time, Pallas kernels for 0%

commit v1 on v0

v1 whole, which is shorter than its diff:
```python
import functools

import jax
import jax.numpy as jnp
from jax import lax
from jax.experimental import pallas as pl
from jax.experimental.pallas import tpu as pltpu
from jax.sharding import PartitionSpec as P

MESH = pl.DeviceIdType.MESH
F32 = jnp.float32
BF16 = jnp.bfloat16
NQ = 4
TILE = 512
N_TILE = 4
Y_OF = ((0, 1), (3, 2))
OFFSETS = [(dx, dy) for dx in range(4) for dy in range(4) if (dx, dy) != (0, 0)]


def split(value):
    high = value.astype(BF16)
    return high, (value - high.astype(F32)).astype(BF16)


def order():
    return [2 * Y_OF[b][a] + x for b in range(2) for a in range(2) for x in range(2)]


def place():
    row, col = lax.axis_index("row"), lax.axis_index("col")
    return row // 2, row % 2, col // 2, col % 2, row, col


def device(x, y, core):
    return {"row": (x // 2) * 2 + core, "col": y * 2 + x % 2}


def kernel(
    trail, low, cross, pinv, tgt, out,
    r_hi, r_lo, stage, slab, acc, lw_hi, lw_lo, in1, in2, in3,
    cross_v, pinv_v, tgt_v, pcp, wl_hi, wl_lo, wr_hi, wr_lo, tw,
    stage_sem, small_sem, send_sem, recv_sem, pass_send, pass_recv, b_send, b_recv, out_sem,
):
    x_hi, core, y, x_lo, row, col = place()
    x = 2 * x_hi + x_lo
    rows = r_hi.shape[0]

    def stage_copy(pos, slot):
        qi, rel, hi = pos // 4, (pos // 2) % 2, pos % 2
        src_row = hi * 2 + (core + rel) % 2
        return pltpu.make_async_copy(
            trail.at[:, src_row * NQ + qi, 0, :], stage.at[slot], stage_sem.at[slot]
        )

    n_stage = stage.shape[0]
    smalls = [
        pltpu.make_async_copy(pinv, pinv_v, small_sem.at[0]),
        pltpu.make_async_copy(cross, cross_v, small_sem.at[1]),
        pltpu.make_async_copy(tgt, tgt_v, small_sem.at[2]),
    ]
    for copy in smalls:
        copy.start()
    for pos in range(n_stage):
        stage_copy(pos, pos).start()

    barrier = pltpu.get_barrier_semaphore()
    for dx, dy in OFFSETS:
        pl.semaphore_signal(
            barrier, inc=1, device_id=device((x + dx) % 4, (y + dy) % 4, core), device_id_type=MESH
        )
    pl.semaphore_signal(barrier, inc=1, device_id=device(x, y, 1 - core), device_id_type=MESH)
    pl.semaphore_wait(barrier, len(OFFSETS) + 1)

    my_slab = slab.at[:, 0, x_hi, pl.ds(pl.multiple_of(col * 96, 96), 96), :]

    def send_low(qi, carry):
        pltpu.make_async_copy(
            low.at[qi, col], my_slab.at[qi], recv_sem.at[qi, x_hi]
        ).start()
        for dx, dy in OFFSETS:
            x2, y2 = (x + dx) % 4, (y + dy) % 4
            pltpu.make_async_remote_copy(
                src_ref=low.at[qi, y2 * 2 + x2 % 2],
                dst_ref=my_slab.at[qi],
                send_sem=send_sem.at[qi],
                recv_sem=recv_sem.at[qi, x_hi],
                device_id=device(x2, y2, core),
                device_id_type=MESH,
            ).start()
        return carry

    lax.fori_loop(0, NQ, send_low, 0)

    for copy in smalls:
        copy.wait()
    exact = functools.partial(
        jnp.dot, preferred_element_type=F32, precision=lax.Precision.HIGHEST
    )
    pcp[...] = exact(exact(pinv_v[1], cross_v[...]), pinv_v[0])
    half = pcp.shape[0]
    left_t = jnp.concatenate([-pinv_v[0].T, pcp[...].T], axis=1)
    wl_hi[...], wl_lo[...] = split(left_t)
    wr_hi[...], wr_lo[...] = split(-pinv_v[1].T)
    own = pl.ds(pl.multiple_of(col * 48, 48), 48)
    own_rows = jnp.concatenate(
        [
            jnp.concatenate([pinv_v[0, own, :], -pcp[own, :]], axis=0),
            jnp.concatenate([jnp.zeros((48, half), F32), pinv_v[1, own, :]], axis=0),
        ],
        axis=1,
    )
    own_hi, own_lo = split(own_rows)
    tw_t = jnp.concatenate(
        [own_hi.astype(F32), own_lo.astype(F32), own_hi.astype(F32)], axis=0
    ).T.astype(BF16)
    for g, c in enumerate(order()):
        for panel in range(2):
            tw[pl.ds(g * 96 + panel * 48, 48), :] = tw_t[panel * half + c * 48 : panel * half + c * 48 + 48]

    acc_flat = acc.reshape(2 * half, rows)

    def start_target(t, carry):
        at = pl.ds(pl.multiple_of(t * TILE, TILE), TILE)
        value = jnp.concatenate([tgt_v[0, :, at], tgt_v[1, :, at]], axis=0)
        high, lowv = split(value)
        rhs = jnp.concatenate([high, high, lowv], axis=0)
        acc_flat[:, at] = jnp.dot(tw[...], rhs, preferred_element_type=F32)
        return carry

    lax.fori_loop(0, N_TILE, start_target, 0)

    def take_stage(pos, carry):
        slot = lax.rem(pos, n_stage)
        stage_copy(pos, slot).wait()
        high, lowv = split(stage[slot])
        at = pl.ds(pl.multiple_of(pos * 128, 128), 128)
        r_hi[:, at] = high
        r_lo[:, at] = lowv

        @pl.when(pos + n_stage < 16)
        def _():
            stage_copy(pos + n_stage, slot).start()

        return carry

    lax.fori_loop(0, 16, take_stage, 0)

    def pass_on(qi, hi):
        return pltpu.make_async_remote_copy(
            src_ref=slab.at[qi, 0, hi],
            dst_ref=slab.at[qi, 1, hi],
            send_sem=pass_send.at[qi, hi],
            recv_sem=pass_recv.at[qi, hi],
            device_id=device(x, y, 1 - core),
            device_id_type=MESH,
        )

    def times_w(qi, rel):
        value = jnp.concatenate([slab[qi, rel, 0], slab[qi, rel, 1]], axis=1)
        high, lowv = split(value)
        at = pl.ds(rel * 256, 256)
        dot = functools.partial(jnp.dot, preferred_element_type=F32)
        left = dot(
            jnp.concatenate([wl_hi[...], wl_lo[...], wl_hi[...]], axis=1),
            jnp.concatenate([high, high, lowv], axis=0),
        )
        right = dot(
            jnp.concatenate([wr_hi[...], wr_lo[...], wr_hi[...]], axis=1),
            jnp.concatenate([high[half:], high[half:], lowv[half:]], axis=0),
        )
        for panel, part in enumerate((left, right)):
            part_hi, part_lo = split(part)
            for g, c in enumerate(order()):
                to = pl.ds(g * 96 + panel * 48, 48)
                lw_hi[to, at] = part_hi[c * 48 : c * 48 + 48]
                lw_lo[to, at] = part_lo[c * 48 : c * 48 + 48]

    def prepare(qi):
        for hi in range(2):
            pltpu.make_async_copy(slab.at[qi, 0, hi], slab.at[qi, 0, hi], recv_sem.at[qi, hi]).wait()
            pass_on(qi, hi).start()
        times_w(qi, 0)
        for hi in range(2):
            pass_on(qi, hi).wait_recv()
        times_w(qi, 1)

    def multiply(qi, t):
        at = pl.ds(pl.multiple_of(t * TILE, TILE), TILE)
        depth = pl.ds(pl.multiple_of(qi * 512, 512), 512)
        lhs = jnp.concatenate([lw_hi[...], lw_lo[...], lw_hi[...]], axis=1)
        high = r_hi[at, depth]
        rhs = jnp.concatenate([high, high, r_lo[at, depth]], axis=1)
        acc_flat[:, at] += lax.dot_general(
            lhs, rhs, (((1,), (1,)), ((), ())), preferred_element_type=F32
        )

    def chunk(qi, carry):
        prepare(qi)

        def tile(t, inner):
            multiply(qi, t)
            return inner

        return lax.fori_loop(0, N_TILE, tile, carry)

    lax.fori_loop(0, NQ - 1, chunk, 0)

    b = y // 2
    a = (y + b) % 2
    x_nbr = device(2 * x_hi + 1 - x_lo, y, core)
    a_nbr = device(x, 3 * b + (1 - 2 * b) * (1 - a), core)
    b_nbr = device(x, 3 * (1 - b) + (2 * b - 1) * a, core)
    every = slice(None)
    sends = (
        ((every, every, 1 - x_lo, 0), (every, 1 - a, x_lo, 0), (1 - b, a, x_lo, 0)),
        ((every, 1 - a, every, 1), (1 - b, a, every, 1), (b, a, 1 - x_lo, 1)),
        ((1 - b, every, every, 2), (b, every, 1 - x_lo, 2), (b, 1 - a, x_lo, 2)),
    )
    keeps = (
        ((every, every, x_lo, 0), (every, a, x_lo, 0), (b, a, x_lo, 0)),
        ((every, a, every, 1), (b, a, every, 1), (b, a, x_lo, 1)),
        ((b, every, every, 2), (b, every, x_lo, 2), (b, a, x_lo, 2)),
    )
    partners = ((x_nbr, a_nbr, b_nbr), (a_nbr, b_nbr, x_nbr), (b_nbr, x_nbr, a_nbr))
    landing = (in1, in2, in3)

    def hop(stage_no, part, t):
        at = pl.ds(pl.multiple_of(t * TILE, TILE), TILE)
        into = landing[stage_no]
        return pltpu.make_async_remote_copy(
            src_ref=acc.at[(*sends[part][stage_no], every, at)],
            dst_ref=into.at[part, ..., at],
            send_sem=b_send.at[stage_no, part, t],
            recv_sem=b_recv.at[stage_no, part, t],
            device_id=partners[part][stage_no],
            device_id_type=MESH,
        )

    def add(stage_no, part, t):
        at = pl.ds(pl.multiple_of(t * TILE, TILE), TILE)
        where = (*keeps[part][stage_no], every, at)
        acc[where] += landing[stage_no][part, ..., at]

    prepare(NQ - 1)

    def last(t, carry):
        multiply(NQ - 1, t)
        for part in range(3):
            hop(0, part, t).start()
        return carry

    lax.fori_loop(0, N_TILE, last, 0)

    for stage_no in range(2):

        def onward(t, carry, stage_no=stage_no):
            for part in range(3):
                hop(stage_no, part, t).wait_recv()
                add(stage_no, part, t)
                hop(stage_no + 1, part, t).start()
            return carry

        lax.fori_loop(0, N_TILE, onward, 0)

    def out_copy(part, t):
        at = pl.ds(pl.multiple_of(t * TILE, TILE), TILE)
        return pltpu.make_async_copy(
            acc.at[b, a, x_lo, part, :, at], out.at[part, :, at], out_sem.at[part, t]
        )

    def finish(t, carry):
        for part in range(3):
            hop(2, part, t).wait_recv()
            add(2, part, t)
            out_copy(part, t).start()
        return carry

    lax.fori_loop(0, N_TILE, finish, 0)

    def drain(t, carry):
        for part in range(3):
            for stage_no in range(3):
                hop(stage_no, part, t).wait_send()
            out_copy(part, t).wait()
        return carry

    lax.fori_loop(0, N_TILE, drain, 0)

    def drain_low(qi, carry):
        sent = slab.at[pl.ds(0, 1), pl.ds(0, 1), :, pl.ds(0, 720), :]
        pltpu.make_async_copy(sent, sent, send_sem.at[qi]).wait()
        for hi in range(2):
            pass_on(qi, hi).wait_send()
        return carry

    lax.fori_loop(0, NQ, drain_low, 0)


def per_device(trailing, lower_trail, lower_cross, panel_inverse, target):
    rows, n_q, _, block = trailing.shape
    width = target.shape[2]
    half = lower_cross.shape[0]
    low = jnp.swapaxes(lower_trail, 2, 3)
    tgt = jnp.transpose(target, (1, 2, 0))
    hbm = pl.BlockSpec(memory_space=pl.ANY)
    dma = pltpu.SemaphoreType.DMA
    out = pl.pallas_call(
        kernel,
        out_shape=jax.ShapeDtypeStruct((3, 32, rows), F32),
        in_specs=[hbm] * 5,
        out_specs=hbm,
        scratch_shapes=[
            pltpu.VMEM((rows, n_q * block), BF16),
            pltpu.VMEM((rows, n_q * block), BF16),
            pltpu.VMEM((4, rows, block), F32),
            pltpu.VMEM((NQ, 2, 2, 2 * half, block), F32),
            pltpu.VMEM((2, 2, 2, 3, 32, rows), F32),
            pltpu.VMEM((2 * half, 4 * block), BF16),
            pltpu.VMEM((2 * half, 4 * block), BF16),
            pltpu.VMEM((3, 2, 2, 32, rows), F32),
            pltpu.VMEM((3, 2, 32, rows), F32),
            pltpu.VMEM((3, 32, rows), F32),
            pltpu.VMEM((half, half), F32),
            pltpu.VMEM((2, half, half), F32),
            pltpu.VMEM((2, width, rows), F32),
            pltpu.VMEM((half, half), F32),
            pltpu.VMEM((half, 2 * half), BF16),
            pltpu.VMEM((half, 2 * half), BF16),
            pltpu.VMEM((half, half), BF16),
            pltpu.VMEM((half, half), BF16),
            pltpu.VMEM((2 * half, 6 * width), BF16),
            dma((4,)),
            dma((3,)),
            dma((NQ,)),
            dma((NQ, 2)),
            dma((NQ, 2)),
            dma((NQ, 2)),
            dma((3, 3, N_TILE)),
            dma((3, 3, N_TILE)),
            dma((3, N_TILE)),
        ],
        compiler_params=pltpu.CompilerParams(
            collective_id=0, has_side_effects=True, vmem_limit_bytes=64 * 1024 * 1024 - 128 * 1024
        ),
    )(trailing, low, lower_cross, panel_inverse, tgt)
    return jnp.transpose(out.reshape(2, width, rows), (2, 0, 1))


def solution(mesh):
    placed = (
        P(("copy", "row"), None, "col", None),
        P(("copy", "row"), None, None, "col"),
        P(),
        P(),
        P(("copy", "row"), None, "col"),
    )
    return jax.shard_map(
        per_device,
        mesh=mesh,
        in_specs=placed,
        out_specs=P(("copy", "row"), None, "col"),
        check_vma=False,
    )
```

time: 370 us -> 95.2 us (0.26); the launches traced: 364 us -> 94.7 us
  blocking collectives: 110 us -> 0 us
  Pallas kernels: 0 us -> 92.7 us
  waiting for transfers between devices: 71.8 us -> 0 us
  matrix products: 65.3 us -> 0 us
  other arithmetic: 55.3 us -> 0 us
  local copies, waits for them, and re-layouts: 47.3 us -> 2.06 us
  starting transfers between devices: 14.1 us -> 0 us
    all_to_all x3 -> x0, blocking collectives: 110 us -> none  [the longest x1 41.8 us: sent_and_summed(): parts = lax.all_to_all(cut_along(array, dim, count), axis, 0, 0, tiled=True)]
    pallas_call x0 -> x1, Pallas kernels: none -> 92.7 us  [per_device(): pl.pallas_call(kernel, out_shape=jax.ShapeDtypeStruct((3, 32, rows), F32)...]
    all_to_all x3 -> x0, waiting for transfers between devices: 71.8 us -> none  [the longest x2 36.7 us: sent_to_all(): lax.all_to_all(jnp.broadcast_to(array[None], (count, *array.shape)), axis...]
    dot_general x4 -> x0, matrix products: 65.3 us -> none  [matmul(): jnp.dot(first, second, preferred_element_type=jnp.float32, precision=prec...]
    unnamed x1 -> x0, other arithmetic: 50 us -> none
    reshape x2 -> x0, local copies, waits for them, and re-layouts: 21.9 us -> none  [the longest x1 18 us: per_device(): trail_flat = trailing.reshape(row_count, trailing.shape[1] * block_cols)]
    all_to_all x3 -> x0, starting transfers between devices: 14.1 us -> none  [the longest x2 9.68 us: sent_to_all(): lax.all_to_all(jnp.broadcast_to(array[None], (count, *array.shape)), axis...]
    all_to_all x2 -> x0, local copies, waits for them, and re-layouts: 7.76 us -> none  [the longest x1 7.65 us: sent_to_all(): lax.all_to_all(jnp.broadcast_to(array[None], (count, *array.shape)), axis...]
  transfers between devices with their start and end apart: 3 -> 0, of which waited for: 3 -> 0; matrix products, arithmetic and copies ran while one was open for 20% -> 0% of each run, Pallas kernels for 0% -> 0%
where the time goes in v1:
time: 95.2 us; the launch traced here: 94.7 us
  Pallas kernels  92.7 us (97%)
  local copies, waits for them, and re-layouts  2.06 us (2%)
    pallas_call x1, Pallas kernels, per_device(): pl.pallas_call(kernel, out_shape=jax.ShapeDtypeStruct((3, 32, rows), F32)...  92.7 us
    unnamed x1, local copies, waits for them, and re-layouts  2.06 us

profile of v1, /device:TPU:0, one launch (start us, length us, event | category | flops | bytes accessed | tf_op | source)
XLA Modules:
  0.0 94.7 jit_solution(15563379747951023496)
XLA Ops:
  0.0 92.7 %shard_map.55 = f32[3,32,2048]{2,1,0:T(8,128)} custom-call(f32[2048,16,1,128]{3,2,1,0:T(1,128)} %trail.1, f32[4,8,96,128]{3,2,1,0:T(8,128)} %bitcast.6, f32[384,384]{1,0:T(8,128)} %cross.1, f32[2,384,384]{2,1,0:T(8,128)} %pinv.1, f32[2,48,2048]{2,1,0:T(8,128)} %bitcast.7), custom_call_target="tpu_custom_call" | custom-call | tf_op jit(solution)/shard_map/pallas_call | solution.py:307
  92.7 2.1 %copy.7 = f32[2048,2,48]{0,2,1:T(8,128)} copy(f32[2048,2,48]{0,2,1:T(8,128)} %bitcast.5) | data formatting | bytes 1572864

commit v2 on v0

v2 whole, which is shorter than its diff:
```python
import functools

import jax
import jax.numpy as jnp
from jax import lax
from jax.experimental import pallas as pl
from jax.experimental.pallas import tpu as pltpu
from jax.sharding import PartitionSpec as P

MESH = pl.DeviceIdType.MESH
F32 = jnp.float32
BF16 = jnp.bfloat16
NQ = 4
TILE = 512
N_TILE = 4
LEFT, RIGHT = 0, 1
Y_OF = ((0, 1), (3, 2))
ORDERS = (("xab", "abx", "bxa"), ("xab", "abx", "bxa"))
OFFSETS = [(dx, dy) for dx in range(4) for dy in range(4) if (dx, dy) != (0, 0)]
OWNERS = [2 * Y_OF[b][a] + x for b in range(2) for a in range(2) for x in range(2)]


def split(value):
    high = value.astype(BF16)
    return high, (value - high.astype(F32)).astype(BF16)


def device(x, y, core):
    return {"row": (x // 2) * 2 + core, "col": y * 2 + x % 2}


def owner_major(value):
    return jnp.concatenate([value[48 * c : 48 * c + 48] for c in OWNERS], axis=0)


def three(high, low):
    return jnp.concatenate([high, low, high], axis=1)


def kernel(
    trail, low, cross, pinv, tgt, out,
    r_hi, r_lo, stage, slab, acc, lw_hi, lw_lo, in1, in2, in3,
    cross_v, pinv_v, tgt_v, pcp, w_left, w_right, tw,
    stage_sem, small_sem, low_send, low_recv, pass_send, pass_recv, b_send, b_recv,
):
    row, col = lax.axis_index("row"), lax.axis_index("col")
    x_hi, core, y, x_lo = row // 2, row % 2, col // 2, col % 2
    x = 2 * x_hi + x_lo
    rows = r_hi.shape[0]
    half = pcp.shape[0]

    def peer(dx, dy):
        return device((x + dx) % 4, (y + dy) % 4, core)

    partner = device(x, y, 1 - core)

    def remote(src, dst, send, recv, to):
        return pltpu.make_async_remote_copy(
            src_ref=src, dst_ref=dst, send_sem=send, recv_sem=recv, device_id=to, device_id_type=MESH
        )

    def wait_bytes(ref, sem):
        pltpu.make_async_copy(ref, ref, sem).wait()

    barrier = pltpu.get_barrier_semaphore()
    for dx, dy in OFFSETS:
        pl.semaphore_signal(barrier, inc=1, device_id=peer(dx, dy), device_id_type=MESH)
    pl.semaphore_signal(barrier, inc=1, device_id=partner, device_id_type=MESH)

    def stage_copy(pos, slot):
        qi, rel, hi = pos // 4, (pos // 2) % 2, pos % 2
        src_row = hi * 2 + (core + rel) % 2
        return pltpu.make_async_copy(
            trail.at[:, src_row * NQ + qi, 0, :], stage.at[slot], stage_sem.at[slot]
        )

    def span(c):
        return pl.ds(pl.multiple_of(c * 96, 96), 96)

    n_stage = stage.shape[0]
    smalls = [
        pltpu.make_async_copy(pinv, pinv_v, small_sem.at[0]),
        pltpu.make_async_copy(cross, cross_v, small_sem.at[1]),
        pltpu.make_async_copy(tgt, tgt_v, small_sem.at[2]),
    ]
    for copy in smalls:
        copy.start()
    for pos in range(n_stage):
        stage_copy(pos, pos).start()
    def take_stage(pos, carry):
        slot = lax.rem(pos, n_stage)
        stage_copy(pos, slot).wait()
        high, lowv = split(stage[slot])
        at = pl.ds(pl.multiple_of(pos * 128, 128), 128)
        r_hi[:, at] = high
        r_lo[:, at] = lowv

        @pl.when(pos + n_stage < 16)
        def _():
            stage_copy(pos + n_stage, slot).start()

        return carry

    pl.semaphore_wait(barrier, len(OFFSETS) + 1)

    mine_at = slab.at[:, 0, x_hi, span(col)]

    def send_low(qi, carry):
        pltpu.make_async_copy(
            low.at[qi, col], mine_at.at[qi], low_recv.at[y // 2, qi, x_hi]
        ).start()
        for dx, dy in OFFSETS:
            x2, y2 = (x + dx) % 4, (y + dy) % 4
            remote(
                low.at[qi, y2 * 2 + x2 % 2], mine_at.at[qi],
                low_send.at[qi], low_recv.at[y // 2, qi, x_hi], device(x2, y2, core),
            ).start()
        return carry

    lax.fori_loop(0, NQ, send_low, 0)

    for copy in smalls:
        copy.wait()

    exact = functools.partial(
        jnp.dot, preferred_element_type=F32, precision=lax.Precision.HIGHEST
    )
    pcp[...] = exact(exact(pinv_v[1], cross_v[...]), pinv_v[0])
    w_left[...] = three(
        *split(owner_major(jnp.concatenate([-pinv_v[0].T, pcp[...].T], axis=1)))
    )
    w_right[...] = three(*split(owner_major(-pinv_v[1].T)))
    own = pl.ds(pl.multiple_of(col * 48, 48), 48)
    own_rows = jnp.concatenate(
        [
            jnp.concatenate([pinv_v[0, own, :], -pcp[own, :]], axis=0),
            jnp.concatenate([jnp.zeros((48, half), F32), pinv_v[1, own, :]], axis=0),
        ],
        axis=1,
    )
    own_hi, own_lo = split(own_rows)
    tw_t = jnp.concatenate(
        [own_hi.astype(F32), own_lo.astype(F32), own_hi.astype(F32)], axis=0
    ).T
    for panel in range(2):
        tw[pl.ds(panel * half, half), :] = owner_major(
            tw_t[panel * half : (panel + 1) * half]
        ).astype(BF16)

    acc_flat = acc.reshape(2 * half, rows)

    def start_target(t, carry):
        at = pl.ds(pl.multiple_of(t * TILE, TILE), TILE)
        high, lowv = split(jnp.concatenate([tgt_v[0, :, at], tgt_v[1, :, at]], axis=0))
        rhs = jnp.concatenate([high, high, lowv], axis=0)
        acc_flat[:, at] = jnp.dot(tw[...], rhs, preferred_element_type=F32)
        return carry

    lax.fori_loop(0, N_TILE, start_target, 0)

    def pass_on(panel, qi, hi):
        part = pl.ds(panel * half, half)
        return remote(
            slab.at[qi, 0, hi, part], slab.at[qi, 1, hi, part],
            pass_send.at[panel, qi, hi], pass_recv.at[panel, qi, hi], partner,
        )

    def take(panel, qi):
        for hi in range(2):
            wait_bytes(slab.at[qi, 0, hi, pl.ds(0, half)], low_recv.at[panel, qi, hi])
            pass_on(panel, qi, hi).start()

    def take_passed(panel, qi):
        for hi in range(2):
            pass_on(panel, qi, hi).wait_recv()

    def times_w(panel, qi):
        part = pl.ds(panel * half, half) if panel == RIGHT else slice(None)
        value = jnp.concatenate(
            [slab[qi, rel, hi, part] for rel in range(2) for hi in range(2)], axis=1
        )
        high, lowv = split(value)
        lhs = (w_left, w_right)[panel]
        product = jnp.dot(
            lhs[...], jnp.concatenate([high, high, lowv], axis=0), preferred_element_type=F32
        )
        to = pl.ds(panel * half, half)
        lw_hi[to, :], lw_lo[to, :] = split(product)

    def multiply(panels, qi, t):
        at = pl.ds(pl.multiple_of(t * TILE, TILE), TILE)
        depth = pl.ds(pl.multiple_of(qi * 512, 512), 512)
        to = pl.ds(panels[0] * half, len(panels) * half)
        lhs = three(lw_hi[to, :], lw_lo[to, :])
        high = r_hi[at, depth]
        rhs = jnp.concatenate([high, high, r_lo[at, depth]], axis=1)
        acc_flat[to, at] += lax.dot_general(
            lhs, rhs, (((1,), (1,)), ((), ())), preferred_element_type=F32
        )

    b = y // 2
    a = (y + b) % 2
    mine = {"b": b, "a": a, "x": x_lo}
    across = {
        "x": device(2 * x_hi + 1 - x_lo, y, core),
        "a": device(x, 3 * b + (1 - 2 * b) * (1 - a), core),
        "b": device(x, 3 * (1 - b) + (2 * b - 1) * a, core),
    }

    def block(panel, stage_no, part, send):
        index = []
        for pair in "bax":
            turn = ORDERS[panel][part].index(pair)
            if turn > stage_no:
                index.append(slice(None))
            else:
                index.append(1 - mine[pair] if send and turn == stage_no else mine[pair])
        return (panel, *index, part, slice(None))

    landing = (in1, in2, in3)

    def hop(panel, stage_no, part, t):
        at = pl.ds(pl.multiple_of(t * TILE, TILE), TILE)
        return remote(
            acc.at[(*block(panel, stage_no, part, True), at)],
            landing[stage_no].at[panel, part, ..., at],
            b_send.at[panel, stage_no, part, t],
            b_recv.at[panel, stage_no, part, t],
            across[ORDERS[panel][part][stage_no]],
        )

    def onward(panel, stage_no, t):
        at = pl.ds(pl.multiple_of(t * TILE, TILE), TILE)
        for part in range(3):
            hop(panel, stage_no, part, t).wait_recv()
            where = (*block(panel, stage_no, part, False), at)
            acc[where] += landing[stage_no][panel, part, ..., at]
            hop(panel, stage_no + 1, part, t).start()

    def finish(panel, t):
        at = pl.ds(pl.multiple_of(t * TILE, TILE), TILE)
        for part in range(3):
            hop(panel, 2, part, t).wait_recv()
            out[panel, part, :, at] = acc[panel, b, a, x_lo, part, :, at] + in3[panel, part, :, at]

    def tiles(body):
        def step(t, carry):
            body(t)
            return carry

        lax.fori_loop(0, N_TILE, step, 0)

    def start_hops(panel, t):
        for part in range(3):
            hop(panel, 0, part, t).start()

    def chunk(qi, carry):
        take(RIGHT, qi)
        take(LEFT, qi)
        for panel in (RIGHT, LEFT):
            take_passed(panel, qi)
            times_w(panel, qi)
        tiles(lambda t: multiply((LEFT, RIGHT), qi, t))
        return carry

    lax.fori_loop(0, 16, take_stage, 0)
    lax.fori_loop(0, NQ - 1, chunk, 0)

    def end(panel):
        def body(t):
            multiply((panel,), NQ - 1, t)
            start_hops(panel, t)

        return body

    final = NQ - 1
    take(RIGHT, final)
    take(LEFT, final)
    take_passed(RIGHT, final)
    times_w(RIGHT, final)
    tiles(end(RIGHT))
    take_passed(LEFT, final)
    times_w(LEFT, final)
    tiles(end(LEFT))
    for stage_no in range(2):
        for panel in (RIGHT, LEFT):
            tiles(lambda t, panel=panel, stage_no=stage_no: onward(panel, stage_no, t))
    for panel in (RIGHT, LEFT):
        tiles(lambda t, panel=panel: finish(panel, t))

    def drain(t):
        for panel in range(2):
            for part in range(3):
                for stage_no in range(3):
                    hop(panel, stage_no, part, t).wait_send()

    tiles(drain)

    def drain_low(qi, carry):
        wait_bytes(slab.at[pl.ds(0, 1), pl.ds(0, 1), :, pl.ds(0, 720)], low_send.at[qi])
        for panel in range(2):
            for hi in range(2):
                pass_on(panel, qi, hi).wait_send()
        return carry

    lax.fori_loop(0, NQ, drain_low, 0)


def per_device(trailing, lower_trail, lower_cross, panel_inverse, target):
    rows, n_q, _, block = trailing.shape
    width = target.shape[2]
    half = lower_cross.shape[0]
    low = jnp.swapaxes(lower_trail, 2, 3)
    tgt = jnp.transpose(target, (1, 2, 0))
    hbm = pl.BlockSpec(memory_space=pl.ANY)
    dma = pltpu.SemaphoreType.DMA
    out = pl.pallas_call(
        kernel,
        out_shape=pltpu.VMEM((2, 3, 16, rows), F32),
        in_specs=[hbm] * 5,
        out_specs=pl.BlockSpec(memory_space=pltpu.VMEM),
        scratch_shapes=[
            pltpu.VMEM((rows, n_q * block), BF16),
            pltpu.VMEM((rows, n_q * block), BF16),
            pltpu.VMEM((4, rows, block), F32),
            pltpu.VMEM((NQ, 2, 2, 2 * half, block), F32),
            pltpu.VMEM((2, 2, 2, 2, 3, 16, rows), F32),
            pltpu.VMEM((2 * half, 4 * block), BF16),
            pltpu.VMEM((2 * half, 4 * block), BF16),
            pltpu.VMEM((2, 3, 2, 2, 16, rows), F32),
            pltpu.VMEM((2, 3, 2, 16, rows), F32),
            pltpu.VMEM((2, 3, 16, rows), F32),
            pltpu.VMEM((half, half), F32),
            pltpu.VMEM((2, half, half), F32),
            pltpu.VMEM((2, width, rows), F32),
            pltpu.VMEM((half, half), F32),
            pltpu.VMEM((half, 6 * half), BF16),
            pltpu.VMEM((half, 3 * half), BF16),
            pltpu.VMEM((2 * half, 6 * width), BF16),
            dma((4,)),
            dma((3,)),
            dma((NQ,)),
            dma((2, NQ, 2)),
            dma((2, NQ, 2)),
            dma((2, NQ, 2)),
            dma((2, 3, 3, N_TILE)),
            dma((2, 3, 3, N_TILE)),
        ],
        compiler_params=pltpu.CompilerParams(
            collective_id=0, has_side_effects=True, vmem_limit_bytes=56 * 1024 * 1024
        ),
    )(trailing, low, lower_cross, panel_inverse, tgt)
    return jnp.transpose(out.reshape(2, width, rows), (2, 0, 1))


def solution(mesh):
    placed = (
        P(("copy", "row"), None, "col", None),
        P(("copy", "row"), None, None, "col"),
        P(),
        P(),
        P(("copy", "row"), None, "col"),
    )
    return jax.shard_map(
        per_device,
        mesh=mesh,
        in_specs=placed,
        out_specs=P(("copy", "row"), None, "col"),
        check_vma=False,
    )
```

time: 370 us -> 92 us (0.25); the launches traced: 364 us -> 91.8 us
  blocking collectives: 110 us -> 0 us
  Pallas kernels: 0 us -> 90.9 us
  waiting for transfers between devices: 71.8 us -> 0 us
  matrix products: 65.3 us -> 0 us
  other arithmetic: 55.3 us -> 0 us
  local copies, waits for them, and re-layouts: 47.3 us -> 0.88 us
  starting transfers between devices: 14.1 us -> 0 us
    all_to_all x3 -> x0, blocking collectives: 110 us -> none  [the longest x1 41.8 us: sent_and_summed(): parts = lax.all_to_all(cut_along(array, dim, count), axis, 0, 0, tiled=True)]
    pallas_call x0 -> x1, Pallas kernels: none -> 90.9 us  [per_device(): pl.pallas_call(kernel, out_shape=pltpu.VMEM((2, 3, 16, rows), F32), in_sp...]
    all_to_all x3 -> x0, waiting for transfers between devices: 71.8 us -> none  [the longest x2 36.7 us: sent_to_all(): lax.all_to_all(jnp.broadcast_to(array[None], (count, *array.shape)), axis...]
    dot_general x4 -> x0, matrix products: 65.3 us -> none  [matmul(): jnp.dot(first, second, preferred_element_type=jnp.float32, precision=prec...]
    unnamed x1 -> x0, other arithmetic: 50 us -> none
    reshape x2 -> x0, local copies, waits for them, and re-layouts: 21.9 us -> none  [the longest x1 18 us: per_device(): trail_flat = trailing.reshape(row_count, trailing.shape[1] * block_cols)]
    all_to_all x3 -> x0, starting transfers between devices: 14.1 us -> none  [the longest x2 9.68 us: sent_to_all(): lax.all_to_all(jnp.broadcast_to(array[None], (count, *array.shape)), axis...]
    all_to_all x2 -> x0, local copies, waits for them, and re-layouts: 7.76 us -> none  [the longest x1 7.65 us: sent_to_all(): lax.all_to_all(jnp.broadcast_to(array[None], (count, *array.shape)), axis...]
  transfers between devices with their start and end apart: 3 -> 0, of which waited for: 3 -> 0; matrix products, arithmetic and copies ran while one was open for 20% -> 0% of each run, Pallas kernels for 0% -> 0%
where the time goes in v2:
time: 92 us; the launch traced here: 91.8 us
  Pallas kernels  90.9 us (99%)
    pallas_call x1, Pallas kernels, per_device(): pl.pallas_call(kernel, out_shape=pltpu.VMEM((2, 3, 16, rows), F32), in_sp...  90.9 us

profile of v2, /device:TPU:0, one launch (start us, length us, event | category | flops | bytes accessed | tf_op | source)
XLA Modules:
  0.0 91.8 jit_solution(16523240285398205471)
XLA Ops:
  0.0 90.9 %shard_map.55 = f32[2,3,16,2048]{3,2,1,0:T(8,128)S(1)} custom-call(f32[2048,16,1,128]{3,2,1,0:T(1,128)} %trail.1, f32[4,8,96,128]{3,2,1,0:T(8,128)} %bitcast.6, f32[384,384]{1,0:T(8,128)} %cross.1, f32[2,384,384]{2,1,0:T(8,128)} %pinv.1, f32[2,48,2048]{2,1,0:T(8,128)} %bitcast.7), custom_call_target="tpu_custom_call" | custom-call | tf_op jit(solution)/shard_map/pallas_call | solution.py:317
  90.9 0.9 copy.7

commit v3 on v2

--- a/solution.py
+++ b/solution.py
@@ -107,13 +107,13 @@
 
     def send_low(qi, carry):
         pltpu.make_async_copy(
-            low.at[qi, col], mine_at.at[qi], low_recv.at[y // 2, qi, x_hi]
+            low.at[qi, col], mine_at.at[qi], low_recv.at[qi, y]
         ).start()
         for dx, dy in OFFSETS:
             x2, y2 = (x + dx) % 4, (y + dy) % 4
             remote(
                 low.at[qi, y2 * 2 + x2 % 2], mine_at.at[qi],
-                low_send.at[qi], low_recv.at[y // 2, qi, x_hi], device(x2, y2, core),
+                low_send, low_recv.at[qi, y], device(x2, y2, core),
             ).start()
         return carry
 
@@ -158,21 +158,23 @@
 
     lax.fori_loop(0, N_TILE, start_target, 0)
 
-    def pass_on(panel, qi, hi):
-        part = pl.ds(panel * half, half)
-        return remote(
-            slab.at[qi, 0, hi, part], slab.at[qi, 1, hi, part],
-            pass_send.at[panel, qi, hi], pass_recv.at[panel, qi, hi], partner,
-        )
+    def piece(qi, rel, ys):
+        return slab.at[qi, rel, :, pl.ds(192 * ys, 192)]
+
+    def pass_on(qi, ys):
+        return remote(piece(qi, 0, ys), piece(qi, 1, ys), pass_send, pass_recv.at[qi, ys], partner)
+
+    def sources(panel):
+        return 2 * panel, 2 * panel + 1
 
     def take(panel, qi):
-        for hi in range(2):
-            wait_bytes(slab.at[qi, 0, hi, pl.ds(0, half)], low_recv.at[panel, qi, hi])
-            pass_on(panel, qi, hi).start()
+        for ys in sources(panel):
+            wait_bytes(piece(qi, 0, ys), low_recv.at[qi, ys])
+            pass_on(qi, ys).start()
 
     def take_passed(panel, qi):
-        for hi in range(2):
-            pass_on(panel, qi, hi).wait_recv()
+        for ys in sources(panel):
+            pass_on(qi, ys).wait_recv()
 
     def times_w(panel, qi):
         part = pl.ds(panel * half, half) if panel == RIGHT else slice(None)
@@ -224,23 +226,23 @@
         return remote(
             acc.at[(*block(panel, stage_no, part, True), at)],
             landing[stage_no].at[panel, part, ..., at],
-            b_send.at[panel, stage_no, part, t],
-            b_recv.at[panel, stage_no, part, t],
+            b_send,
+            b_recv.at[panel, stage_no, t],
             across[ORDERS[panel][part][stage_no]],
         )
 
     def onward(panel, stage_no, t):
         at = pl.ds(pl.multiple_of(t * TILE, TILE), TILE)
+        wait_bytes(landing[stage_no].at[panel, ..., at], b_recv.at[panel, stage_no, t])
         for part in range(3):
-            hop(panel, stage_no, part, t).wait_recv()
             where = (*block(panel, stage_no, part, False), at)
             acc[where] += landing[stage_no][panel, part, ..., at]
             hop(panel, stage_no + 1, part, t).start()
 
     def finish(panel, t):
         at = pl.ds(pl.multiple_of(t * TILE, TILE), TILE)
+        wait_bytes(in3.at[panel, ..., at], b_recv.at[panel, 2, t])
         for part in range(3):
-            hop(panel, 2, part, t).wait_recv()
             out[panel, part, :, at] = acc[panel, b, a, x_lo, part, :, at] + in3[panel, part, :, at]
 
     def tiles(body):
@@ -255,15 +257,24 @@
             hop(panel, 0, part, t).start()
 
     def chunk(qi, carry):
-        take(RIGHT, qi)
-        take(LEFT, qi)
         for panel in (RIGHT, LEFT):
             take_passed(panel, qi)
             times_w(panel, qi)
-        tiles(lambda t: multiply((LEFT, RIGHT), qi, t))
+
+        def tile(t):
+            multiply((LEFT, RIGHT), qi, t)
+
+            @pl.when(t == 2)
+            def _():
+                take(RIGHT, qi + 1)
+                take(LEFT, qi + 1)
+
+        tiles(tile)
         return carry
 
     lax.fori_loop(0, 16, take_stage, 0)
+    take(RIGHT, 0)
+    take(LEFT, 0)
     lax.fori_loop(0, NQ - 1, chunk, 0)
 
     def end(panel):
@@ -274,8 +285,6 @@
         return body
 
     final = NQ - 1
-    take(RIGHT, final)
-    take(LEFT, final)
     take_passed(RIGHT, final)
     times_w(RIGHT, final)
     tiles(end(RIGHT))
@@ -288,22 +297,9 @@
     for panel in (RIGHT, LEFT):
         tiles(lambda t, panel=panel: finish(panel, t))
 
-    def drain(t):
-        for panel in range(2):
-            for part in range(3):
-                for stage_no in range(3):
-                    hop(panel, stage_no, part, t).wait_send()
-
-    tiles(drain)
-
-    def drain_low(qi, carry):
-        wait_bytes(slab.at[pl.ds(0, 1), pl.ds(0, 1), :, pl.ds(0, 720)], low_send.at[qi])
-        for panel in range(2):
-            for hi in range(2):
-                pass_on(panel, qi, hi).wait_send()
-        return carry
-
-    lax.fori_loop(0, NQ, drain_low, 0)
+    wait_bytes(acc_flat.at[pl.ds(0, 7 * half // 4)], b_send)
+    wait_bytes(slab.at[pl.ds(0, 2), :, :, pl.ds(0, 720)], low_send)
+    wait_bytes(slab.at[pl.ds(0, 2)], pass_send)
 
 
 def per_device(trailing, lower_trail, lower_cross, panel_inverse, target):
@@ -339,12 +335,12 @@
             pltpu.VMEM((2 * half, 6 * width), BF16),
             dma((4,)),
             dma((3,)),
-            dma((NQ,)),
-            dma((2, NQ, 2)),
-            dma((2, NQ, 2)),
-            dma((2, NQ, 2)),
-            dma((2, 3, 3, N_TILE)),
-            dma((2, 3, 3, N_TILE)),
+            dma(()),
+            dma((NQ, 4)),
+            dma(()),
+            dma((NQ, 4)),
+            dma(()),
+            dma((2, 3, N_TILE)),
         ],
         compiler_params=pltpu.CompilerParams(
             collective_id=0, has_side_effects=True, vmem_limit_bytes=56 * 1024 * 1024

time: 92 us -> 90 us (0.978)
  Pallas kernels: 90.9 us -> 88.7 us
    pallas_call x1, Pallas kernels: 90.9 us -> 88.7 us  [per_device(): pl.pallas_call(kernel, out_shape=pltpu.VMEM((2, 3, 16, rows), F32), in_sp...]
where the time goes in v3:
time: 90 us; the launch traced here: 89.6 us
  Pallas kernels  88.7 us (99%)
    pallas_call x1, Pallas kernels, per_device(): pl.pallas_call(kernel, out_shape=pltpu.VMEM((2, 3, 16, rows), F32), in_sp...  88.7 us

profile of v3, /device:TPU:0, one launch (start us, length us, event | category | flops | bytes accessed | tf_op | source)
XLA Modules:
  0.0 89.6 jit_solution(6249694613947409841)
XLA Ops:
  0.0 88.7 %shard_map.55 = f32[2,3,16,2048]{3,2,1,0:T(8,128)S(1)} custom-call(f32[2048,16,1,128]{3,2,1,0:T(1,128)} %trail.1, f32[4,8,96,128]{3,2,1,0:T(8,128)} %bitcast.6, f32[384,384]{1,0:T(8,128)} %cross.1, f32[2,384,384]{2,1,0:T(8,128)} %pinv.1, f32[2,48,2048]{2,1,0:T(8,128)} %bitcast.7), custom_call_target="tpu_custom_call" | custom-call | tf_op jit(solution)/shard_map/pallas_call | solution.py:313
  88.7 0.9 copy.7

commit v4 on v3

--- a/solution.py
+++ b/solution.py
@@ -264,9 +264,12 @@
         def tile(t):
             multiply((LEFT, RIGHT), qi, t)
 
+            @pl.when(t == 1)
+            def _():
+                take(RIGHT, qi + 1)
+
             @pl.when(t == 2)
             def _():
-                take(RIGHT, qi + 1)
                 take(LEFT, qi + 1)
 
         tiles(tile)

time: 90 us -> 89.1 us (0.990)
  no operation moved by 1% of the time
where the time goes in v4:
time: 89.1 us; the launch traced here: 89 us
  Pallas kernels  88.1 us (99%)
    pallas_call x1, Pallas kernels, per_device(): pl.pallas_call(kernel, out_shape=pltpu.VMEM((2, 3, 16, rows), F32), in_sp...  88.1 us

profile of v4, /device:TPU:0, one launch (start us, length us, event | category | flops | bytes accessed | tf_op | source)
XLA Modules:
  0.0 89.0 jit_solution(2589476981120442821)
XLA Ops:
  0.0 88.1 %shard_map.55 = f32[2,3,16,2048]{3,2,1,0:T(8,128)S(1)} custom-call(f32[2048,16,1,128]{3,2,1,0:T(1,128)} %trail.1, f32[4,8,96,128]{3,2,1,0:T(8,128)} %bitcast.6, f32[384,384]{1,0:T(8,128)} %cross.1, f32[2,384,384]{2,1,0:T(8,128)} %pinv.1, f32[2,48,2048]{2,1,0:T(8,128)} %bitcast.7), custom_call_target="tpu_custom_call" | custom-call | tf_op jit(solution)/shard_map/pallas_call | solution.py:316
  88.1 0.9 copy.7
